TPU v7x, 32 devices: a whole 2x2x4 slice. The times are simulated.
32 devices in a mesh: cfg: 2 (over core), tp: 8 (over z, x), dp: 2 (over y).
Axes of the slice: x: 2, y: 2, z: 4, core: 2. Of those that a mesh axis runs over, the one named last changes fastest.
Arguments:
- tokens: bfloat16 [4096, 512], P('dp'), parts along dimension 0, may hold values from -6 to 6
- conditions: float32 [4, 256], P(('dp', 'cfg')), parts along dimension 0, may hold values from -6 to 6
- ada_block: bfloat16 [256, 3072], P(None, 'tp'), may hold values from -1 to 1
- ada_final: bfloat16 [256, 1024], P(None, 'tp'), may hold values from -1 to 1
- qkv_weight: bfloat16 [512, 3, 512], P(None, None, 'tp'), may hold values from -0.25 to 0.25
- out_weight: bfloat16 [512, 512], P('tp'), may hold values from -0.25 to 0.25
- up_weight: bfloat16 [512, 2048], P(None, 'tp'), may hold values from -0.25 to 0.25
- down_weight: bfloat16 [2048, 512], P('tp'), may hold values from -0.125 to 0.125
- final_weight: bfloat16 [512, 64], replicated, may hold values from -0.25 to 0.25
Outputs:
- guided: float32 [4096, 64], P('dp'), parts along dimension 0
There are 2 independent parts, one for each index of `dp`. A program takes and returns all parts, laid end to end along the dimension named above; an argument that names none is the same for every part. Nothing has to cross between parts.
All inputs are finite; a program needn't handle non-finite values.
Results may differ from a plain program's by a relative error of at most 0.02.
Values may be sent and summed in bfloat16 or wider, within the bound.
A program may use at most 128 MiB of HBM per device.

v0:
```python
import jax
import jax.numpy as jnp
from jax import lax
from jax.sharding import PartitionSpec as P

HEAD_SIZE = 64
guidance = 4.0
epsilon = 1e-06


def layer_norm(values):
    average = jnp.mean(values, -1, keepdims=True)
    centred = values - average
    spread = jnp.mean(centred * centred, -1, keepdims=True)
    return centred * lax.rsqrt(spread + epsilon)


def modulate(stream, scales, shifts):
    return (layer_norm(stream) * (1.0 + scales) + shifts).astype(jnp.bfloat16)


def attend(projected):
    token_count = projected.shape[0]
    local_width = projected.shape[2]
    local_heads = local_width // HEAD_SIZE
    per_head = projected.reshape(token_count, 3, local_heads, HEAD_SIZE)
    scores = jnp.einsum(
        "thd,shd->hts", per_head[:, 0], per_head[:, 1], preferred_element_type=jnp.float32
    ) * HEAD_SIZE ** (-0.5)
    softmaxed = jax.nn.softmax(scores, axis=-1)
    values_f = per_head[:, 2].astype(jnp.float32)
    head_out = jnp.einsum("hts,shd->thd", softmaxed, values_f)
    return head_out.reshape(token_count, local_width).astype(jnp.bfloat16)


def local(
    tokens,
    conditions,
    ada_block,
    ada_final,
    qkv_weight,
    out_weight,
    up_weight,
    down_weight,
    final_weight,
):
    model_width = tokens.shape[1]
    signal = jax.nn.silu(conditions).astype(jnp.bfloat16)
    block_local = jnp.dot(signal, ada_block, preferred_element_type=jnp.float32)[0]
    final_local = jnp.dot(signal, ada_final, preferred_element_type=jnp.float32)[0]
    shifts, final_mod = (
        lax.all_gather(block_local, "tp", axis=0, tiled=True),
        lax.all_gather(final_local, "tp", axis=0, tiled=True),
    )
    shifts = shifts.reshape(6, model_width)
    stream = tokens.astype(jnp.float32)
    normed = modulate(stream, shifts[1], shifts[0])
    projected = jnp.einsum(
        "td,dke->tke", normed, qkv_weight, preferred_element_type=jnp.float32
    ).astype(jnp.bfloat16)
    head_out = attend(projected)
    attended = lax.psum(
        jnp.dot(head_out, out_weight, preferred_element_type=jnp.float32).astype(jnp.bfloat16), "tp"
    ).astype(jnp.float32)
    stream = stream + shifts[2] * attended
    normed = modulate(stream, shifts[4], shifts[3])
    upward = jnp.dot(normed, up_weight, preferred_element_type=jnp.float32)
    hidden = jax.nn.gelu(upward, approximate=True).astype(jnp.bfloat16)
    mlp_out = lax.psum(
        jnp.dot(hidden, down_weight, preferred_element_type=jnp.float32).astype(jnp.bfloat16), "tp"
    ).astype(jnp.float32)
    stream = stream + shifts[5] * mlp_out
    final_mod = final_mod.reshape(2, model_width)
    final_in = modulate(stream, final_mod[1], final_mod[0])
    predicted = jnp.dot(final_in, final_weight, preferred_element_type=jnp.float32)
    is_cond = lax.axis_index("cfg") == 0
    weighting = jnp.where(is_cond, guidance, 1.0 - guidance).astype(jnp.float32)
    return lax.psum((weighting * predicted).astype(jnp.bfloat16), "cfg").astype(jnp.float32)


def solution(mesh):
    placed = (
        P("dp", None),
        P(("dp", "cfg"), None),
        P(None, "tp"),
        P(None, "tp"),
        P(None, None, "tp"),
        P("tp", None),
        P(None, "tp"),
        P("tp", None),
        P(),
    )
    return jax.shard_map(
        local, mesh=mesh, in_specs=placed, out_specs=P("dp", None), check_vma=False
    )
```

profile of v0, /device:TPU:0, one launch (start us, length us, event | category | flops | bytes accessed | tf_op | source)
XLA Modules:
  0.0 313.4 jit_solution(2466030839063625285)
XLA Ops:
  6.5 0.0 copy-start
  6.5 0.0 copy-start.1
  6.5 0.0 copy-start.8
  6.5 0.0 all-reduce.4.cloned.1.call-start
  6.5 1.2 convolution_bitcast_fusion
  7.8 27.8 %all-gather = f32[8,1,384]{2,1,0:T(1,128)S(1)} all-gather(f32[1,1,384]{2,1,0:T(1,128)S(1)} %convolution_bitcast_fusion), channel_id=1, replica_groups=mesh['cfg'=2,'tp'=8,'dp'=2] {'tp'}, dimensions={0}, use_global_device_ids=true | all-gather | bytes 13824 | tf_op jit(solution)/shard_map/all_gather | solution.py:52
  35.6 1.9 convert_reduce_fusion
  37.6 2.5 fusion.8
  40.1 0.0 copy-done.1
  40.1 0.0 copy-done.8
  40.1 1.2 fusion.28
  41.3 0.1 convert_bitcast_fusion
  41.4 8.1 %multiply_reduce_fusion = (f32[2048]{0:T(1024)S(1)}, f32[2048,2048]{0,1:T(8,128)}) fusion(bf16[2048,3,1,64]{0,3,1,2:T(8,128)(2,1)S(1)} %convert_bitcast_fusion), kind=kOutput, calls=%fused_computation.3 | convolution fusion | flops 545257472 | bytes 17309696 | tf_op jit(solution)/shard_map/thd,shd->hts/dot_general | solution.py:27
  49.5 0.0 copy-start.9
  49.5 8.6 %fusion.2 = f32[2048]{0:T(1024)S(1)} fusion(f32[2048,2048]{0,1:T(8,128)} %get-tuple-element.14, f32[2048]{0:T(1024)S(1)} %get-tuple-element.13), kind=kLoop, calls=%fused_computation.4 | loop fusion | flops 12580864 | bytes 16793600 | tf_op jit(solution)/shard_map/reduce_sum | solution.py:30
  58.1 0.0 copy-done.9
  58.1 8.9 %convolution_convert_fusion.1 = bf16[2048,512]{1,0:T(8,128)(2,1)} fusion(bf16[64,512]{1,0:T(8,128)(2,1)S(1)} %copy-done.9, f32[2048,2048]{0,1:T(8,128)} %get-tuple-element.14, f32[2048]{0:T(1024)S(1)} %fusion.2, f32[2048]{0:T(1024)S(1)} %get-tuple-element.13, bf16[2048,3,1,64]{0,3,1,2:T(8,128)(2,1)S(1)} %convert_bitcast_fusion), kind=kOutput, calls=%fused_computation.24 | convolution fusion | flops 684851200 | bytes 19218432 | tf_op jit(solution)/shard_map/dot_general | solution.py:63
  67.0 0.0 all-reduce.4.cloned.1.call-update
  67.0 0.2 all-reduce.6.cloned.1.call-start
  67.3 101.6 %all-reduce.4.cloned.1.call-done = bf16[2048,512]{1,0:T(8,128)(2,1)} async-done(((bf16[2048,512]{1,0:T(8,128)(2,1)}), bf16[2048,512]{1,0:T(8,128)(2,1)}) %all-reduce.4.cloned.1.call-update) | async-done | bytes 2097168 | tf_op jit(solution)/shard_map/psum | solution.py:62
  168.9 0.0 copy-start.2
  168.9 0.0 copy-start.7
  168.9 2.5 fusion.12
  171.4 0.0 copy-done.2
  171.4 1.2 multiply_reduce_fusion.2
  172.6 0.0 copy-done
  172.6 0.0 copy-done.7
  172.6 0.0 copy-start.5
  172.6 0.0 copy-start.6
  172.6 5.1 %convolution_convert_fusion = bf16[2048,512]{1,0:T(8,128)(2,1)} fusion(bf16[256,512]{1,0:T(8,128)(2,1)S(1)} %copy-done, bf16[512,256]{1,0:T(8,128)(2,1)S(1)} %copy-done.7, bf16[2048,512]{1,0:T(8,128)(2,1)} %all-reduce.4.cloned.1.call-done, bf16[2048,512]{1,0:T(8,128)(2,1)S(1)} %copy-done.1, f32[512]{0:T(512)S(1)} %get-tuple-element.6, ...), kind=kOutput, calls=%fused_computation.23 | convolution fusion | flops 1088946176 | bytes 6838272 | tf_op jit(solution)/shard_map/dot_general | solution.py:70
  177.7 0.0 all-reduce.6.cloned.1.call-update
  177.8 0.0 all-reduce.8.cloned.1.call-start
  177.8 0.0 copy-done.5
  177.8 0.0 copy-done.6
  177.9 0.1 convolution_bitcast_fusion.1
  178.0 19.2 %all-gather.1 = f32[8,1,128]{2,1,0:T(1,128)S(1)} all-gather(f32[1,1,128]{2,1,0:T(1,128)S(1)} %convolution_bitcast_fusion.1), channel_id=1, replica_groups=mesh['cfg'=2,'tp'=8,'dp'=2] {'tp'}, dimensions={0}, use_global_device_ids=true | all-gather | bytes 4608 | tf_op jit(solution)/shard_map/all_gather | solution.py:53
  197.2 82.3 %all-reduce.6.cloned.1.call-done = bf16[2048,512]{1,0:T(8,128)(2,1)} async-done(((bf16[2048,512]{1,0:T(8,128)(2,1)}), bf16[2048,512]{1,0:T(8,128)(2,1)}) %all-reduce.6.cloned.1.call-update) | async-done | bytes 2097168 | tf_op jit(solution)/shard_map/psum | solution.py:69
  279.5 0.0 copy-start.3
  279.5 3.5 %fusion.45 = f32[2048]{0:T(1024)S(1)} fusion(bf16[2048,512]{1,0:T(8,128)(2,1)} %all-reduce.6.cloned.1.call-done, f32[512]{0:T(512)S(1)} %get-tuple-element.5, bf16[2048,512]{1,0:T(8,128)(2,1)} %all-reduce.4.cloned.1.call-done, f32[512]{0:T(512)S(1)} %get-tuple-element.10, bf16[2048,512]{1,0:T(8,128)(2,1)S(1)} %copy-done.1), kind=kLoop, calls=%fused_computation.58 | loop fusion | flops 8386560 | bytes 6303744 | tf_op jit(solution)/shard_map/reduce_sum | solution.py:12
  283.1 0.0 copy-start.10
  283.1 0.0 copy-done.3
  283.1 0.0 copy-done.4
  283.1 1.6 multiply_reduce_fusion.1
  284.7 0.0 copy-done.10
  284.7 2.7 fusion.13
  287.4 0.0 all-reduce.8.cloned.1.call-update
  287.4 17.7 %all-reduce.8.cloned.1.call-done = bf16[2048,64]{0,1:T(8,128)(2,1)} async-done(((bf16[2048,64]{0,1:T(8,128)(2,1)}), bf16[2048,64]{0,1:T(8,128)(2,1)}) %all-reduce.8.cloned.1.call-update) | async-done | bytes 262160 | tf_op jit(solution)/shard_map/psum | solution.py:78
  305.1 1.8 convert_element_type.68
  (9 shorter events, 0.0 us)
Async XLA Ops:
  6.5 166.1 %copy-start = (bf16[256,512]{1,0:T(8,128)(2,1)S(1)}, bf16[256,512]{1,0:T(8,128)(2,1)}, u32[]{:S(2)}) copy-start(bf16[256,512]{1,0:T(8,128)(2,1)} %param.16) | copy-start | bytes 786436
  6.5 33.5 %copy-start.1 = (bf16[2048,512]{1,0:T(8,128)(2,1)S(1)}, bf16[2048,512]{1,0:T(8,128)(2,1)}, u32[]{:S(2)}) copy-start(bf16[2048,512]{1,0:T(8,128)(2,1)} %param.9) | copy-start | bytes 6291460
  6.5 33.6 %copy-start.8 = (bf16[512,3,64]{0,2,1:T(8,128)(2,1)S(1)}, bf16[512,3,64]{0,2,1:T(8,128)(2,1)}, u32[]{:S(2)}) copy-start(bf16[512,3,64]{0,2,1:T(8,128)(2,1)} %param.13) | copy-start | bytes 589828
  6.5 162.3 %all-reduce.4.cloned.1.call-start = ((), (), s32[]{:S(2)}) async-start(), calls=%async_computation | async-start | bytes 4194304 | tf_op jit(solution)/shard_map/psum | solution.py:62
  49.5 8.6 %copy-start.9 = (bf16[64,512]{1,0:T(8,128)(2,1)S(1)}, bf16[64,512]{1,0:T(8,128)(2,1)}, u32[]{:S(2)}) copy-start(bf16[64,512]{1,0:T(8,128)(2,1)} %param.14) | copy-start | bytes 196612
  67.0 212.5 %all-reduce.6.cloned.1.call-start = ((), (), s32[]{:S(2)}) async-start(), calls=%async_computation.1 | async-start | bytes 4194304 | tf_op jit(solution)/shard_map/psum | solution.py:69
  168.9 2.5 copy-start.2
  168.9 3.7 %copy-start.7 = (bf16[512,256]{1,0:T(8,128)(2,1)S(1)}, bf16[512,256]{1,0:T(8,128)(2,1)}, u32[]{:S(2)}) copy-start(bf16[512,256]{1,0:T(8,128)(2,1)} %param.15) | copy-start | bytes 786436
  172.6 5.2 %copy-start.5 = (bf16[256,128]{1,0:T(8,128)(2,1)S(1)}, bf16[256,128]{1,0:T(8,128)(2,1)}, u32[]{:S(2)}) copy-start(bf16[256,128]{1,0:T(8,128)(2,1)} %param.12) | copy-start | bytes 196612
  172.6 5.2 %copy-start.6 = (f32[1,256]{1,0:T(1,128)S(1)}, f32[1,256]{1,0:T(1,128)}, u32[]{:S(2)}) copy-start(f32[1,256]{1,0:T(1,128)} %param.10) | copy-start | bytes 3076
  177.8 127.3 %all-reduce.8.cloned.1.call-start = ((), (), s32[]{:S(2)}) async-start(), calls=%async_computation.2 | async-start | bytes 524288 | tf_op jit(solution)/shard_map/psum | solution.py:78
  279.5 3.6 %copy-start.3 = (bf16[2048,512]{1,0:T(8,128)(2,1)S(1)}, bf16[2048,512]{1,0:T(8,128)(2,1)}, u32[]{:S(2)}) copy-start(bf16[2048,512]{1,0:T(8,128)(2,1)} %all-reduce.4.cloned.1.call-done) | copy-start | bytes 6291460
  279.5 3.6 %copy-start.4 = (bf16[2048,512]{1,0:T(8,128)(2,1)S(1)}, bf16[2048,512]{1,0:T(8,128)(2,1)}, u32[]{:S(2)}) copy-start(bf16[2048,512]{1,0:T(8,128)(2,1)} %all-reduce.6.cloned.1.call-done) | copy-start | bytes 6291460
  283.1 1.7 copy-start.10
Sparse Core Ops, SparseCore 0:
  67.2 101.6 all-reduce.3
  177.9 101.5 all-reduce.5
  287.5 17.5 all-reduce.7
where the time goes:
time: 314 us; the launch traced here: 313 us
  waiting for transfers between devices  202 us (64%)
  blocking collectives  47.1 us (15%)
  matrix products  27.4 us (9%)
  other arithmetic  23.7 us (8%)
  between operations  13.3 us (4%)
    psum x1, waiting for transfers between devices, local(): lax.psum(jnp.dot(head_out, out_weight, preferred_element_type=jnp.float32...  102 us
    psum x1, waiting for transfers between devices, local(): lax.psum(jnp.dot(hidden, down_weight, preferred_element_type=jnp.float32)...  82.3 us
    all_gather x1, blocking collectives, local(): lax.all_gather(block_local, 'tp', axis=0, tiled=True)  27.8 us
    all_gather x1, blocking collectives, local(): lax.all_gather(final_local, 'tp', axis=0, tiled=True)  19.2 us
    psum x1, waiting for transfers between devices, local(): lax.psum((weighting * predicted).astype(jnp.bfloat16), 'cfg')  17.7 us
    dot_general x1, matrix products, local(): jnp.dot(head_out, out_weight, preferred_element_type=jnp.float32)  8.92 us
    reduce_sum x1, other arithmetic, attend(): softmaxed = jax.nn.softmax(scores, axis=-1)  8.58 us
    dot_general x1, matrix products, attend(): jnp.einsum('thd,shd->hts', per_head[:, 0], per_head[:, 1], preferred_elem...  8.09 us
  transfers between devices with their start and end apart: 3, of which 3 were waited for; matrix products, arithmetic and copies ran while one was open for 0% of the time, Pallas kernels for 0%

commit v1 on v0

--- a/solution.py
+++ b/solution.py
@@ -59,8 +59,12 @@
         "td,dke->tke", normed, qkv_weight, preferred_element_type=jnp.float32
     ).astype(jnp.bfloat16)
     head_out = attend(projected)
-    attended = lax.psum(
-        jnp.dot(head_out, out_weight, preferred_element_type=jnp.float32).astype(jnp.bfloat16), "tp"
+    attended = jnp.sum(
+        lax.all_gather(
+            jnp.dot(head_out, out_weight, preferred_element_type=jnp.float32).astype(jnp.bfloat16),
+            "tp",
+        ),
+        axis=0,
     ).astype(jnp.float32)
     stream = stream + shifts[2] * attended
     normed = modulate(stream, shifts[4], shifts[3])

time: 314 us -> 448 us (1.43)
  waiting for transfers between devices: 202 us -> 327 us
  other arithmetic: 23.7 us -> 34.2 us
    all_gather x0 -> x1, waiting for transfers between devices: none -> 227 us  [local(): lax.all_gather(jnp.dot(head_out, out_weight, preferred_element_type=jnp.f...]
    psum x1 -> x0, waiting for transfers between devices: 102 us -> none  [local(): lax.psum(jnp.dot(head_out, out_weight, preferred_element_type=jnp.float32...]
    reduce_sum x0 -> x1, other arithmetic: none -> 10.5 us  [local(): jnp.sum(lax.all_gather(jnp.dot(head_out, out_weight, preferred_element_ty...]
where the time goes in v1:
time: 448 us
  waiting for transfers between devices  327 us (73%)
  blocking collectives  46 us (10%)
  other arithmetic  34.2 us (8%)
  matrix products  27.3 us (6%)
  between operations  13.3 us (3%)
    all_gather x1, waiting for transfers between devices, local(): lax.all_gather(jnp.dot(head_out, out_weight, preferred_element_type=jnp.f...  227 us
    psum x1, waiting for transfers between devices, local(): lax.psum(jnp.dot(hidden, down_weight, preferred_element_type=jnp.float32)...  82.3 us
    all_gather x1, blocking collectives, local(): lax.all_gather(block_local, 'tp', axis=0, tiled=True)  27.8 us
    all_gather x1, blocking collectives, local(): lax.all_gather(final_local, 'tp', axis=0, tiled=True)  18.1 us
    psum x1, waiting for transfers between devices, local(): lax.psum((weighting * predicted).astype(jnp.bfloat16), 'cfg')  17.7 us
    reduce_sum x1, other arithmetic, local(): jnp.sum(lax.all_gather(jnp.dot(head_out, out_weight, preferred_element_ty...  10.5 us
  transfers between devices with their start and end apart: 3, of which 3 were waited for; matrix products, arithmetic and copies ran while one was open for 0% of the time, Pallas kernels for 0%

profile of v1, /device:TPU:0, one launch (start us, length us, event | category | flops | bytes accessed | tf_op | source)
XLA Modules:
  0.0 447.8 jit_solution(7541108120411694951)
XLA Ops:
  6.5 0.0 copy-start
  6.5 0.0 copy-start.1
  6.5 0.0 copy-start.8
  6.5 0.0 all-gather.5.cloned.1.call-start
  6.5 1.2 convolution_bitcast_fusion
  7.8 27.8 %all-gather.1 = f32[8,1,384]{2,1,0:T(1,128)S(1)} all-gather(f32[1,1,384]{2,1,0:T(1,128)S(1)} %convolution_bitcast_fusion), channel_id=1, replica_groups=mesh['cfg'=2,'tp'=8,'dp'=2] {'tp'}, dimensions={0}, use_global_device_ids=true | all-gather | bytes 13824 | tf_op jit(solution)/shard_map/all_gather | solution.py:52
  35.6 1.9 convert_reduce_fusion
  37.6 2.5 fusion.8
  40.1 0.0 copy-done.1
  40.1 0.0 copy-done.8
  40.1 1.2 fusion.28
  41.3 0.1 convert_bitcast_fusion
  41.4 8.1 %multiply_reduce_fusion = (f32[2048]{0:T(1024)S(1)}, f32[2048,2048]{0,1:T(8,128)}) fusion(bf16[2048,3,1,64]{0,3,1,2:T(8,128)(2,1)S(1)} %convert_bitcast_fusion), kind=kOutput, calls=%fused_computation.3 | convolution fusion | flops 545257472 | bytes 17309696 | tf_op jit(solution)/shard_map/thd,shd->hts/dot_general | solution.py:27
  49.5 0.0 copy-start.9
  49.5 8.6 %fusion.2 = f32[2048]{0:T(1024)S(1)} fusion(f32[2048,2048]{0,1:T(8,128)} %get-tuple-element.14, f32[2048]{0:T(1024)S(1)} %get-tuple-element.13), kind=kLoop, calls=%fused_computation.4 | loop fusion | flops 12580864 | bytes 16793600 | tf_op jit(solution)/shard_map/reduce_sum | solution.py:30
  58.1 0.0 copy-done.9
  58.1 8.9 %convolution_convert_fusion.1 = bf16[2048,512]{1,0:T(8,128)(2,1)} fusion(bf16[64,512]{1,0:T(8,128)(2,1)S(1)} %copy-done.9, f32[2048,2048]{0,1:T(8,128)} %get-tuple-element.14, f32[2048]{0:T(1024)S(1)} %fusion.2, f32[2048]{0:T(1024)S(1)} %get-tuple-element.13, bf16[2048,3,1,64]{0,3,1,2:T(8,128)(2,1)S(1)} %convert_bitcast_fusion), kind=kOutput, calls=%fused_computation.24 | convolution fusion | flops 684851200 | bytes 19218432 | tf_op jit(solution)/shard_map/dot_general | solution.py:64
  67.0 0.0 all-gather.5.cloned.1.call-update
  67.0 0.2 all-reduce.3.cloned.1.call-start
  67.3 226.6 %all-gather.5.cloned.1.call-done = bf16[16384,512]{1,0:T(8,128)(2,1)} async-done(((bf16[2048,512]{1,0:T(8,128)(2,1)}), bf16[16384,512]{1,0:T(8,128)(2,1)}) %all-gather.5.cloned.1.call-update) | async-done | bytes 16777232 | tf_op jit(solution)/shard_map/all_gather | solution.py:63
  293.9 10.5 %reduce_sum.78 = bf16[2048,512]{1,0:T(8,128)(2,1)} reduce(bf16[8,2048,512]{2,1,0:T(8,128)(2,1)} %bitcast.48, bf16[]{:T(256)} %constant.38.clone.1), dimensions={0}, to_apply=%region_4.5 | reduce | flops 7340032 | bytes 18874370 | tf_op jit(solution)/shard_map/reduce_sum | solution.py:62
  304.4 0.0 copy-start.2
  304.4 0.0 copy-start.7
  304.4 2.5 fusion.12
  306.9 0.0 copy-done.2
  307.0 1.2 multiply_reduce_fusion.2
  308.1 0.0 copy-done
  308.2 0.0 copy-done.7
  308.2 0.0 copy-start.5
  308.2 0.0 copy-start.6
  308.2 5.1 %convolution_convert_fusion = bf16[2048,512]{1,0:T(8,128)(2,1)} fusion(bf16[256,512]{1,0:T(8,128)(2,1)S(1)} %copy-done, bf16[512,256]{1,0:T(8,128)(2,1)S(1)} %copy-done.7, bf16[2048,512]{1,0:T(8,128)(2,1)} %reduce_sum.78, bf16[2048,512]{1,0:T(8,128)(2,1)S(1)} %copy-done.1, f32[512]{0:T(512)S(1)} %get-tuple-element.6, f32[512]{0:T(512)S(1)} %get-tuple-element.7, ...), kind=kOutput, calls=%fused_computation.23 | convolution fusion | flops 1088946176 | bytes 6838272 | tf_op jit(solution)/shard_map/dot_general | solution.py:74
  313.3 0.0 all-reduce.3.cloned.1.call-update
  313.3 0.0 all-reduce.5.cloned.1.call-start
  313.3 0.0 copy-done.5
  313.3 0.0 copy-done.6
  313.4 0.1 convolution_bitcast_fusion.1
  313.5 18.1 %all-gather.2 = f32[8,1,128]{2,1,0:T(1,128)S(1)} all-gather(f32[1,1,128]{2,1,0:T(1,128)S(1)} %convolution_bitcast_fusion.1), channel_id=1, replica_groups=mesh['cfg'=2,'tp'=8,'dp'=2] {'tp'}, dimensions={0}, use_global_device_ids=true | all-gather | bytes 4608 | tf_op jit(solution)/shard_map/all_gather | solution.py:53
  331.6 82.3 %all-reduce.3.cloned.1.call-done = bf16[2048,512]{1,0:T(8,128)(2,1)} async-done(((bf16[2048,512]{1,0:T(8,128)(2,1)}), bf16[2048,512]{1,0:T(8,128)(2,1)}) %all-reduce.3.cloned.1.call-update) | async-done | bytes 2097168 | tf_op jit(solution)/shard_map/psum | solution.py:73
  413.9 3.5 fusion.45
  417.4 0.0 copy-start.10
  417.5 0.0 copy-done.3
  417.5 0.0 copy-done.4
  417.5 1.6 multiply_reduce_fusion.1
  419.1 0.0 copy-done.10
  419.1 2.7 fusion.13
  421.8 0.0 all-reduce.5.cloned.1.call-update
  421.8 17.7 %all-reduce.5.cloned.1.call-done = bf16[2048,64]{0,1:T(8,128)(2,1)} async-done(((bf16[2048,64]{0,1:T(8,128)(2,1)}), bf16[2048,64]{0,1:T(8,128)(2,1)}) %all-reduce.5.cloned.1.call-update) | async-done | bytes 262160 | tf_op jit(solution)/shard_map/psum | solution.py:82
  439.5 1.8 convert_element_type.70
  (10 shorter events, 0.0 us)
Async XLA Ops:
  6.5 301.6 %copy-start = (bf16[256,512]{1,0:T(8,128)(2,1)S(1)}, bf16[256,512]{1,0:T(8,128)(2,1)}, u32[]{:S(2)}) copy-start(bf16[256,512]{1,0:T(8,128)(2,1)} %param.16) | copy-start | bytes 786436
  6.5 33.5 %copy-start.1 = (bf16[2048,512]{1,0:T(8,128)(2,1)S(1)}, bf16[2048,512]{1,0:T(8,128)(2,1)}, u32[]{:S(2)}) copy-start(bf16[2048,512]{1,0:T(8,128)(2,1)} %param.9) | copy-start | bytes 6291460
  6.5 33.6 %copy-start.8 = (bf16[512,3,64]{0,2,1:T(8,128)(2,1)S(1)}, bf16[512,3,64]{0,2,1:T(8,128)(2,1)}, u32[]{:S(2)}) copy-start(bf16[512,3,64]{0,2,1:T(8,128)(2,1)} %param.13) | copy-start | bytes 589828
  6.5 287.3 %all-gather.5.cloned.1.call-start = ((), (), s32[]{:S(2)}) async-start(), calls=%async_computation.2 | async-start | bytes 18874368 | tf_op jit(solution)/shard_map/all_gather | solution.py:63
  49.5 8.6 %copy-start.9 = (bf16[64,512]{1,0:T(8,128)(2,1)S(1)}, bf16[64,512]{1,0:T(8,128)(2,1)}, u32[]{:S(2)}) copy-start(bf16[64,512]{1,0:T(8,128)(2,1)} %param.14) | copy-start | bytes 196612
  67.0 346.9 %all-reduce.3.cloned.1.call-start = ((), (), s32[]{:S(2)}) async-start(), calls=%async_computation | async-start | bytes 4194304 | tf_op jit(solution)/shard_map/psum | solution.py:73
  304.4 2.5 copy-start.2
  304.4 3.7 copy-start.7
  308.2 5.2 %copy-start.5 = (bf16[256,128]{1,0:T(8,128)(2,1)S(1)}, bf16[256,128]{1,0:T(8,128)(2,1)}, u32[]{:S(2)}) copy-start(bf16[256,128]{1,0:T(8,128)(2,1)} %param.12) | copy-start | bytes 196612
  308.2 5.2 %copy-start.6 = (f32[1,256]{1,0:T(1,128)S(1)}, f32[1,256]{1,0:T(1,128)}, u32[]{:S(2)}) copy-start(f32[1,256]{1,0:T(1,128)} %param.10) | copy-start | bytes 3076
  313.3 126.2 %all-reduce.5.cloned.1.call-start = ((), (), s32[]{:S(2)}) async-start(), calls=%async_computation.1 | async-start | bytes 524288 | tf_op jit(solution)/shard_map/psum | solution.py:82
  413.9 3.6 copy-start.3
  413.9 3.6 copy-start.4
  417.4 1.7 copy-start.10
Sparse Core Ops, SparseCore 0:
  67.2 226.6 all-gather.4
  313.4 100.4 all-reduce.2
  421.9 17.5 all-reduce.4
